TPU v7x, 512 devices: a whole 4x8x8 slice. The times are simulated.
512 devices in a mesh: seq: 8 (over x, core), dp: 8 (over z), tensor: 8 (over y).
Axes of the slice: x: 4, y: 8, z: 8, core: 2. Of those that a mesh axis runs over, the one named last changes fastest.
Arguments:
- queries: bfloat16 [8, 3072, 2048], P('dp', ('seq', 'tensor')), may hold values from -128 to 128
- key_vectors: bfloat16 [8, 3072, 2048], P('dp', ('seq', 'tensor')), may hold values from -6 to 6
- values: bfloat16 [8, 3072, 2048], P('dp', ('seq', 'tensor')), may hold values from -6 to 6
- out_grad: bfloat16 [8, 3072, 2048], P('dp', ('seq', 'tensor')), may hold values from -6 to 6
- positions: int32 [8, 3072], P('dp', 'seq'), may hold values from -1 to 16383, as said below
- sink_logits: float32 [16], P('tensor'), may hold values from -1 to 3
Outputs:
- attended: bfloat16 [8, 3072, 2048], P('dp', ('seq', 'tensor'))
- query_grad: bfloat16 [8, 3072, 2048], P('dp', ('seq', 'tensor'))
- key_grad: bfloat16 [8, 3072, 2048], P('dp', ('seq', 'tensor'))
- value_grad: bfloat16 [8, 3072, 2048], P('dp', ('seq', 'tensor'))
- sink_grad: float32 [16], P('tensor')
Inputs may be any that keep to these rules, and one draw needn't show every extreme that they name: Each document's tokens 0 to 16383 form slabs of 4096 tokens; each slab keeps exactly 512 routed tokens, its first half on one sequence shard of 384 slots and its second half on the next. A shard lists its routed positions in rising order in its first slots and -1 in the slots left over; it holds 128 to 384 routed tokens, and some shard of every document holds 384.
All inputs are finite; a program needn't handle non-finite values.
Results may differ from a plain program's by a relative error of at most 0.02.
Values may be sent and summed in bfloat16 or wider, within the bound.
A program may use at most 64 MiB of HBM per device.

v0:
```python
import jax
import jax.numpy as jnp
from jax import lax
from jax.sharding import PartitionSpec as P

DH = 128


def sent_together(arrays, axis, split_dim, concat_dim, along):
    both = jnp.concatenate(arrays, axis=along)
    whole, at, outs = (
        lax.all_to_all(both, axis, split_axis=split_dim, concat_axis=concat_dim, tiled=True),
        0,
        [],
    )
    for a in arrays:
        outs.append(lax.slice_in_dim(whole, at, at + a.shape[along], axis=along))
        at += a.shape[along]
    return tuple(outs)


def in_one_piece(arrays, axis, dim, along):
    ends, at = ([], 0)
    for a in arrays[:-1]:
        at += a.shape[along]
        ends.append(at)
    both = jnp.concatenate(arrays, axis=along)
    return tuple(jnp.split(lax.all_gather(both, axis, axis=dim, tiled=True), ends, axis=along))


def sent_to_all(x, axis):
    copies = jnp.broadcast_to(x, (lax.axis_size(axis), *x.shape))
    return lax.all_to_all(copies, axis, split_axis=0, concat_axis=0, tiled=True)


def over_copies(x, axis):
    everything = sent_to_all(x, axis)
    return jnp.sum(everything, axis=0)


def block_scores(query_block, query_pos, key_block, key_pos):
    raw_scores = jnp.einsum(
        "ghd,khd->hgk", query_block, key_block, preferred_element_type=jnp.float32
    )
    scores = raw_scores * DH ** (-0.5)
    visible = (key_pos[None, :] <= query_pos[:, None]) & (key_pos[None, :] >= 0)
    return jnp.where(visible[None], scores, -1e30)


def row_stats(query_rows, query_pos, last_slab, key_all, key_pos, sink_logits, key_span):
    head_count = query_rows.shape[1]
    row_count = query_rows.shape[0]
    start_max = jnp.broadcast_to(sink_logits[:, None], (head_count, row_count))
    start_total = jnp.zeros((head_count, row_count), jnp.float32)

    def row_one_block(block, loop_state):
        row_max, row_total = loop_state
        key_block = lax.dynamic_slice_in_dim(key_all, block * key_span, key_span, 0)
        pos_block = lax.dynamic_slice_in_dim(key_pos, block * key_span, key_span, 0)
        scores = block_scores(query_rows, query_pos, key_block, pos_block)
        new_max = jnp.maximum(row_max, jnp.max(scores, axis=2))
        row_total = row_total * jnp.exp(row_max - new_max) + jnp.sum(
            jnp.exp(scores - new_max[:, :, None]), axis=2
        )
        return (new_max, row_total)

    row_max, row_total = lax.fori_loop(0, last_slab + 1, row_one_block, (start_max, start_total))
    return (row_max, row_total + jnp.exp(sink_logits[:, None] - row_max))


def attend_rows(
    query_rows, query_pos, last_slab, key_all, value_all, key_pos, row_max, row_total, key_span
):

    def attend_one_block(block, summed):
        key_block = lax.dynamic_slice_in_dim(key_all, block * key_span, key_span, 0)
        value_block = lax.dynamic_slice_in_dim(value_all, block * key_span, key_span, 0)
        pos_block = lax.dynamic_slice_in_dim(key_pos, block * key_span, key_span, 0)
        scores = block_scores(query_rows, query_pos, key_block, pos_block)
        weights_half = (jnp.exp(scores - row_max[:, :, None]) / row_total[:, :, None]).astype(
            jnp.bfloat16
        )
        return summed + jnp.einsum(
            "hgk,khd->ghd", weights_half, value_block, preferred_element_type=jnp.float32
        )

    summed = lax.fori_loop(
        0, last_slab + 1, attend_one_block, jnp.zeros(query_rows.shape, jnp.float32)
    )
    return summed.astype(jnp.bfloat16)


def query_grads(
    query_rows,
    grad_rows,
    query_pos,
    last_slab,
    key_all,
    value_all,
    key_pos,
    row_max,
    row_total,
    delta_rows,
    key_span,
    key_sums,
    value_sums,
):

    def query_one_block(block, loop_state):
        query_sum, key_state, value_state = loop_state
        key_block = lax.dynamic_slice_in_dim(key_all, block * key_span, key_span, 0)
        value_block = lax.dynamic_slice_in_dim(value_all, block * key_span, key_span, 0)
        pos_block = lax.dynamic_slice_in_dim(key_pos, block * key_span, key_span, 0)
        scores = block_scores(query_rows, query_pos, key_block, pos_block)
        weights_full = jnp.exp(scores - row_max[:, :, None]) / row_total[:, :, None]
        value_dots = jnp.einsum(
            "ghd,khd->hgk", grad_rows, value_block, preferred_element_type=jnp.float32
        )
        score_grad = (weights_full * (value_dots - delta_rows[:, :, None]) * DH ** (-0.5)).astype(
            jnp.bfloat16
        )
        query_sum = query_sum + jnp.einsum(
            "hgk,khd->ghd", score_grad, key_block, preferred_element_type=jnp.float32
        )
        return (query_sum, key_state, value_state)

    start = (jnp.zeros(query_rows.shape, jnp.float32), key_sums, value_sums)
    query_sum, key_sums, value_sums = lax.fori_loop(0, last_slab + 1, query_one_block, start)
    return (query_sum.astype(jnp.bfloat16), key_sums, value_sums)


def key_grads(
    key_rows,
    value_rows,
    key_pos,
    query_all,
    grad_all,
    query_pos_all,
    max_all,
    total_all,
    delta_all,
    first_slab,
    slab_count,
    query_span,
):

    def key_one_block(block, loop_state):
        key_sum, value_sum = loop_state
        query_block = lax.dynamic_slice_in_dim(query_all, block * query_span, query_span, 0)
        grad_block = lax.dynamic_slice_in_dim(grad_all, block * query_span, query_span, 0)
        pos_block = lax.dynamic_slice_in_dim(query_pos_all, block * query_span, query_span, 0)
        max_block = lax.dynamic_slice_in_dim(max_all, block * query_span, query_span, 1)
        total_block = lax.dynamic_slice_in_dim(total_all, block * query_span, query_span, 1)
        delta_block = lax.dynamic_slice_in_dim(delta_all, block * query_span, query_span, 1)
        scores = block_scores(query_block, pos_block, key_rows, key_pos)
        weights_full = jnp.exp(scores - max_block[:, :, None]) / total_block[:, :, None]
        value_dots = jnp.einsum(
            "ghd,khd->hgk", grad_block, value_rows, preferred_element_type=jnp.float32
        )
        score_grad = (weights_full * (value_dots - delta_block[:, :, None]) * DH ** (-0.5)).astype(
            jnp.bfloat16
        )
        key_sum = key_sum + jnp.einsum(
            "hgk,ghd->khd", score_grad, query_block, preferred_element_type=jnp.float32
        )
        value_sum = value_sum + jnp.einsum(
            "hgk,ghd->khd",
            weights_full.astype(jnp.bfloat16),
            grad_block,
            preferred_element_type=jnp.float32,
        )
        return (key_sum, value_sum)

    zeros = jnp.zeros(key_rows.shape, jnp.float32)
    return lax.fori_loop(first_slab, slab_count, key_one_block, (zeros, zeros))


def on_device(queries, key_vectors, values, out_grad, positions, sink_logits):
    queries, key_vectors, values, out_grad = sent_together(
        (queries, key_vectors, values, out_grad), "tensor", 2, 1, 0
    )
    capacity = queries.shape[1]
    features = queries.shape[2]
    head_count = features // DH
    key_span = 2 * capacity
    seq_count = lax.axis_size("seq")
    seq_index = lax.axis_index("seq")
    query_rows = queries[0].reshape(capacity, head_count, DH)
    key_rows = key_vectors[0].reshape(capacity, head_count, DH)
    value_rows = values[0].reshape(capacity, head_count, DH)
    grad_rows = out_grad[0].reshape(capacity, head_count, DH)
    pos_rows = positions[0]
    key_all, value_all, key_pos = (
        *in_one_piece((key_rows, value_rows), "seq", 0, 1),
        lax.all_gather(pos_rows, "seq", axis=0, tiled=True),
    )
    own_slab = seq_index // 2
    groups = (query_rows, grad_rows, pos_rows, own_slab)
    key_sums = None
    value_sums = None
    sink_sum = jnp.zeros((head_count,), jnp.float32)
    group_rows, group_grads, group_pos, last_slab = groups
    row_max, row_total = row_stats(
        group_rows, group_pos, last_slab, key_all, key_pos, sink_logits, key_span
    )
    attended = attend_rows(
        group_rows, group_pos, last_slab, key_all, value_all, key_pos, row_max, row_total, key_span
    )
    delta_rows = jnp.sum(attended.astype(jnp.float32) * group_grads.astype(jnp.float32), axis=2).T
    sink_sum = sink_sum - jnp.sum(
        jnp.exp(sink_logits[:, None] - row_max) / row_total * delta_rows, axis=1
    )
    query_grad, key_sums, value_sums = query_grads(
        group_rows,
        group_grads,
        group_pos,
        last_slab,
        key_all,
        value_all,
        key_pos,
        row_max,
        row_total,
        delta_rows,
        key_span,
        key_sums,
        value_sums,
    )
    results = (attended, query_grad, row_max, row_total, delta_rows)
    attended = results[0]
    query_grad = results[1]
    own_max = results[2]
    own_total = results[3]
    own_delta = results[4]
    query_all, grad_all, query_pos_all = (
        lax.all_gather(query_rows, "seq", axis=0, tiled=True),
        lax.all_gather(grad_rows, "seq", axis=0, tiled=True),
        lax.all_gather(pos_rows, "seq", axis=0, tiled=True),
    )
    max_all, total_all, delta_all = in_one_piece((own_max, own_total, own_delta), "seq", 1, 0)
    key_sum, value_sum = key_grads(
        key_rows,
        value_rows,
        pos_rows,
        query_all,
        grad_all,
        query_pos_all,
        max_all,
        total_all,
        delta_all,
        own_slab,
        seq_count // 2,
        key_span,
    )
    key_grad, value_grad = sent_together(
        (
            key_sum.astype(jnp.bfloat16).reshape(1, capacity, features),
            value_sum.astype(jnp.bfloat16).reshape(1, capacity, features),
        ),
        "tensor",
        1,
        2,
        0,
    )
    attended, query_grad = sent_together(
        (attended.reshape(1, capacity, features), query_grad.reshape(1, capacity, features)),
        "tensor",
        1,
        2,
        0,
    )
    sink_grad = over_copies(sink_sum, ("seq", "dp"))
    return (attended, query_grad, key_grad, value_grad, sink_grad)


def solution(mesh):
    placed = (
        P("dp", ("seq", "tensor"), None),
        P("dp", ("seq", "tensor"), None),
        P("dp", ("seq", "tensor"), None),
        P("dp", ("seq", "tensor"), None),
        P("dp", "seq"),
        P("tensor"),
    )
    return jax.shard_map(
        on_device,
        mesh=mesh,
        in_specs=placed,
        out_specs=(
            P("dp", ("seq", "tensor"), None),
            P("dp", ("seq", "tensor"), None),
            P("dp", ("seq", "tensor"), None),
            P("dp", ("seq", "tensor"), None),
            P("tensor"),
        ),
        check_vma=False,
    )
```

profile of v0, /device:TPU:1, one launch (start us, length us, event | category | flops | bytes accessed | tf_op | source)
XLA Modules:
  0.0 253.4 jit_solution(17397691539322435936)
XLA Ops:
  9.9 3.2 %reshape.243 = bf16[8,2,24576]{2,1,0:T(2,128)(2,1)S(1)} reshape(bf16[2048,4,48]{2,1,0:T(4,128)(2,1)S(1)} %bitcast.139) | data formatting | bytes 1572864
  13.2 27.7 %all_to_all.51 = bf16[8,2,24576]{2,1,0:T(2,128)(2,1)} all-to-all(bf16[8,2,24576]{2,1,0:T(2,128)(2,1)S(1)} %reshape.243), channel_id=1, replica_groups=mesh['seq'=8,'dp'=8,'tensor'=8] {'tensor'}, dimensions={0} | all-to-all | bytes 1572864 | tf_op jit(solution)/shard_map/all_to_all | solution.py:12
  40.8 5.7 %reshape.244 = bf16[2048,4,48]{2,1,0:T(4,128)(2,1)S(1)} reshape(bf16[8,2,24576]{2,1,0:T(2,128)(2,1)} %all_to_all.51) | data formatting | bytes 1572864
  50.0 15.7 %all-gather = s32[1,3072]{1,0:T(1,128)S(1)} all-gather(s32[1,384]{1,0:T(1,128)S(1)} %copy-done.5), channel_id=2, replica_groups=mesh['seq'=8,'dp'=8,'tensor'=8] {'seq'}, dimensions={1}, use_global_device_ids=true | all-gather | bytes 13824 | tf_op jit(solution)/shard_map/all_gather | solution.py:195
  68.9 16.4 %all-gather.5.cloned.1.call-done = bf16[3072,4,128]{2,1,0:T(4,128)(2,1)} async-done(((bf16[384,4,128]{2,1,0:T(4,128)(2,1)}), bf16[3072,4,128]{2,1,0:T(4,128)(2,1)}) %all-gather.5.cloned.1.call-update) | async-done | bytes 3145744 | tf_op jit(solution)/shard_map/all_gather | solution.py:28
  85.3 6.6 %fusion.60 = (bf16[3072,2,128]{2,1,0:T(2,128)(2,1)}, bf16[3072,2,128]{2,1,0:T(2,128)(2,1)S(1)}) fusion(bf16[3072,4,128]{2,1,0:T(4,128)(2,1)} %all-gather.5.cloned.1.call-done), kind=kLoop, calls=%fused_computation.93 | loop fusion | bytes 6291456 | tf_op jit(solution)/shard_map/split | solution.py:28
  93.4 2.6 %while.44 = (s32[]{:T(128)}, f32[2,384]{1,0:T(2,128)S(1)}, f32[2,384]{1,0:T(2,128)S(1)}, s32[]{:T(128)}, s32[3072]{0:T(1024)S(1)}, /*index=5*/s32[1,384]{1,0:T(1...) while((s32[]{:T(128)}, f32[2,384]{1,0:T(2,128)S(1)}, ...), condition=%wide.region_3.4_spmd, body=%wide.region_0.3_spmd.sunk | while | flops 155715840 | bytes 6248631 | solution.py:67
  97.1 3.8 %while.45 = (s32[]{:T(128)}, f32[384,2,128]{0,2,1:T(8,128)S(1)}, s32[]{:T(128)}, bf16[3072,2,128]{2,1,0:T(2,128)(2,1)}, s32[3072]{0:T(1024)S(1)}, /*index=5*/s32...) while((s32[]{:T(128)}, f32[384,2,128]{0,2,1:T(8,128)S(1)}, ...), condition=%wide.region_5.6_spmd, body=%wide.region_4.5_spmd.sunk | while | flops 305627904 | bytes 3167435 | solution.py:87
  98.8 2.1 fusion.96
  102.6 6.4 %while.46 = (s32[]{:T(128)}, f32[384,2,128]{0,2,1:T(8,128)}, s32[]{:T(128)}, bf16[3072,2,128]{2,0,1:T(8,128)(2,1)}, s32[3072]{0:T(1024)S(1)}, /*index=5*/s32[1,3...) while((s32[]{:T(128)}, f32[384,2,128]{0,2,1:T(8,128)}, ...), condition=%wide.region_8.9_spmd, body=%wide.region_7.8_spmd.sunk | while | flops 458392320 | bytes 8478943 | solution.py:128
  105.7 3.2 %fusion.103 = f32[384,2,128]{0,2,1:T(8,128)} fusion(f32[384,2,128]{0,2,1:T(8,128)} %get-tuple-element.1045, f32[2,768,384]{2,1,0:T(8,128)S(1)} %fusion.102, bf16[384,2,128]{2,0,1:T(8,128)(2,1)} %get-tuple-element.1070, f32[2,384]{1,0:T(2,128)S(1)} %get-tuple-element.1071, f32[2,384]{1,0:T(2,128)S(1)} %get-tuple-element.1068, ...), kind=kOutput, calls=%fused_computation.39.clone.1 | convolution fusion | flops 306806784 | bytes 4432900 | tf_op jit(solution)/shard_map/while/body/hgk,khd->ghd/dot_general | solution.py:122
  112.8 47.8 %all-to-all-start.3 = ((f32[64,1,2]{2,1,0:T(1,128)}), f32[64,1,2]{2,1,0:T(1,128)S(1)}, u32[]{:S(2)}, u32[]{:S(2)}) async-start(f32[64,1,2]{2,1,0:T(1,128)} %broadcast_in_dim.76), calls=%async_computation.3 | async-start | bytes 65536 | tf_op jit(solution)/shard_map/all_to_all | solution.py:33
  160.6 13.6 %all_gather.19 = f32[6,3072]{1,0:T(8,128)S(1)} all-gather(f32[6,384]{1,0:T(8,128)S(1)} %pad_maximum_fusion.4), channel_id=1, replica_groups=mesh['seq'=8,'dp'=8,'tensor'=8] {'seq'}, dimensions={1}, use_global_device_ids=true | all-gather | bytes 82944 | tf_op jit(solution)/shard_map/all_gather | solution.py:28
  176.0 6.5 %all-to-all-start.1 = ((bf16[2,384,256]{2,0,1:T(2,128)(2,1)}), bf16[2,384,256]{2,0,1:T(2,128)(2,1)}, u32[]{:S(2)}, u32[]{:S(2)}) async-start(bf16[2,384,256]{2,0,1:T(2,128)(2,1)} %copy.257), calls=%async_computation.1 | async-start | bytes 786432 | tf_op jit(solution)/shard_map/all_to_all | solution.py:12
  183.3 39.1 %while.47 = (s32[]{:T(128)}, f32[384,2,128]{0,2,1:T(8,128)S(1)}, f32[384,2,128]{0,2,1:T(8,128)}, bf16[3072,2,128]{2,1,0:T(2,128)(2,1)}, s32[1,384]{1,0:T(1,128)S...) while((s32[]{:T(128)}, f32[384,2,128]{0,2,1:T(8,128)S(1)}, ...), condition=%wide.region_10.11_spmd, body=%wide.region_9.10_spmd.sunk | while | flops 610075008 | bytes 13244495 | solution.py:175
  187.3 1.8 exponential_divide_fusion.2
  189.1 1.7 fusion.111
  190.9 2.2 fusion.112
  195.4 1.7 constant_dynamic-slice_fusion.16
  197.0 1.8 exponential_divide_fusion.2
  198.9 1.7 fusion.111
  200.6 2.2 fusion.112
  205.1 1.7 constant_dynamic-slice_fusion.16
  206.8 1.8 exponential_divide_fusion.2
  208.7 1.7 fusion.111
  210.4 2.2 fusion.112
  214.9 1.7 constant_dynamic-slice_fusion.16
  216.6 1.8 exponential_divide_fusion.2
  218.4 1.7 fusion.111
  220.2 2.2 fusion.112
  224.6 6.6 %all-to-all-start.2 = ((bf16[2,384,256]{2,0,1:T(2,128)(2,1)}), bf16[2,384,256]{2,0,1:T(2,128)(2,1)S(1)}, u32[]{:S(2)}, u32[]{:S(2)}) async-start(bf16[2,384,256]{2,0,1:T(2,128)(2,1)} %copy.267), calls=%async_computation.2 | async-start | bytes 786432 | tf_op jit(solution)/shard_map/all_to_all | solution.py:12
  234.3 11.1 %all-to-all-done.2 = bf16[2,384,256]{2,0,1:T(2,128)(2,1)S(1)} async-done(((bf16[2,384,256]{2,0,1:T(2,128)(2,1)}), bf16[2,384,256]{2,0,1:T(2,128)(2,1)S(1)}, u32[]{:S(2)}, u32[]{:S(2)}) %all-to-all-start.2) | async-done | bytes 393248 | tf_op jit(solution)/shard_map/all_to_all | solution.py:12
  (152 shorter events, 44.8 us)
Async XLA Ops:
  7.2 78.2 %all-gather.5.cloned.1.call-start = ((), (), s32[]{:S(2)}) async-start(), calls=%async_computation.4 | async-start | bytes 3538944 | tf_op jit(solution)/shard_map/all_gather | solution.py:28
  47.7 2.3 copy-start.5
  49.1 133.3 %all-gather.7.cloned.1.call-start = ((), (), s32[]{:S(2)}) async-start(), calls=%async_computation.5 | async-start | bytes 1769472 | tf_op jit(solution)/shard_map/all_gather | solution.py:235
  49.9 132.5 %all-gather.9.cloned.1.call-start = ((), (), s32[]{:S(2)}) async-start(), calls=%async_computation.6 | async-start | bytes 1769472 | tf_op jit(solution)/shard_map/all_gather | solution.py:236
  68.2 0.7 copy-start
  91.9 1.4 copy-start.12
  96.4 0.7 copy-start.2
  97.1 4.0 %copy-start.1 = (bf16[384,2,128]{2,1,0:T(2,128)(2,1)S(1)}, bf16[384,2,128]{2,1,0:T(2,128)(2,1)}, u32[]{:S(2)}) copy-start(bf16[384,2,128]{2,1,0:T(2,128)(2,1)} %copy-done) | copy-start | bytes 589828
  101.1 1.4 copy-start.4
  101.6 0.9 copy-start.3
  112.8 63.2 %all-to-all-start.3 = ((f32[64,1,2]{2,1,0:T(1,128)}), f32[64,1,2]{2,1,0:T(1,128)S(1)}, u32[]{:S(2)}, u32[]{:S(2)}) async-start(f32[64,1,2]{2,1,0:T(1,128)} %broadcast_in_dim.76), calls=%async_computation.3 | async-start | bytes 65536 | tf_op jit(solution)/shard_map/all_to_all | solution.py:33
  176.0 7.3 %copy-start.6 = (f32[64,1,2]{2,1,0:T(1,128)}, f32[64,1,2]{2,1,0:T(1,128)S(1)}, u32[]{:S(2)}) copy-start(f32[64,1,2]{2,1,0:T(1,128)S(1)} %all-to-all-done.3) | copy-start | bytes 1540
  176.0 48.7 %all-to-all-start.1 = ((bf16[2,384,256]{2,0,1:T(2,128)(2,1)}), bf16[2,384,256]{2,0,1:T(2,128)(2,1)}, u32[]{:S(2)}, u32[]{:S(2)}) async-start(bf16[2,384,256]{2,0,1:T(2,128)(2,1)} %copy.257), calls=%async_computation.1 | async-start | bytes 786432 | tf_op jit(solution)/shard_map/all_to_all | solution.py:12
  183.3 2.3 copy-start.8
  183.3 2.3 copy-start.10
  190.8 2.2 copy-start.9
  190.9 2.2 copy-start.11
  193.1 2.3 copy-start.8
  193.1 2.3 copy-start.10
  200.6 2.2 copy-start.9
  200.6 2.2 copy-start.11
  202.8 2.3 copy-start.8
  202.8 2.3 copy-start.10
  210.4 2.2 copy-start.9
  210.4 2.2 copy-start.11
  212.6 2.3 copy-start.8
  212.6 2.3 copy-start.10
  220.2 2.2 copy-start.9
  220.2 2.2 copy-start.11
  222.4 8.8 %copy-start.7 = (f32[64,1,2]{2,1,0:T(1,128)S(1)}, f32[64,1,2]{2,1,0:T(1,128)}, u32[]{:S(2)}) copy-start(f32[64,1,2]{2,1,0:T(1,128)} %copy-done.6) | copy-start | bytes 1540
  224.6 20.7 %all-to-all-start.2 = ((bf16[2,384,256]{2,0,1:T(2,128)(2,1)}), bf16[2,384,256]{2,0,1:T(2,128)(2,1)S(1)}, u32[]{:S(2)}, u32[]{:S(2)}) async-start(bf16[2,384,256]{2,0,1:T(2,128)(2,1)} %copy.267), calls=%async_computation.2 | async-start | bytes 786432 | tf_op jit(solution)/shard_map/all_to_all | solution.py:12
Sparse Core Ops, SparseCore 0:
  49.2 36.0 all-gather.4
  88.0 29.6 all-gather.6
  120.4 29.9 all-gather.8
where the time goes:
time: 255 us; the launch traced here: 253 us
  starting transfers between devices  61 us (24%)
  blocking collectives  56.9 us (22%)
  local copies, waits for them, and re-layouts  52.1 us (20%)
  matrix products  31.5 us (12%)
  waiting for transfers between devices  27.6 us (11%)
  between operations  14.1 us (6%)
  other arithmetic  9.84 us (4%)
    all_to_all x1, starting transfers between devices, sent_to_all(): return lax.all_to_all(copies, axis, split_axis=0, concat_axis=0, tiled=True)  47.8 us
    all_to_all x1, blocking collectives, sent_together(): lax.all_to_all(both, axis, split_axis=split_dim, concat_axis=concat_dim,...  27.7 us
    all_gather x1, waiting for transfers between devices, in_one_piece(): lax.all_gather(both, axis, axis=dim, tiled=True)  16.4 us
    all_gather x1, blocking collectives, on_device(): lax.all_gather(pos_rows, 'seq', axis=0, tiled=True)  15.7 us
    all_gather x1, blocking collectives, in_one_piece(): lax.all_gather(both, axis, axis=dim, tiled=True)  13.6 us
    all_to_all x2, starting transfers between devices, sent_together(): lax.all_to_all(both, axis, split_axis=split_dim, concat_axis=concat_dim,...  13.1 us
    all_to_all x2, waiting for transfers between devices, sent_together(): lax.all_to_all(both, axis, split_axis=split_dim, concat_axis=concat_dim,...  11.1 us
    dot_general x6, matrix products, block_scores(): jnp.einsum('ghd,khd->hgk', query_block, key_block, preferred_element_type...  10.5 us
  transfers between devices with their start and end apart: 6, of which 2 were waited for; matrix products, arithmetic and copies ran while one was open for 30% of the time, Pallas kernels for 0%

commit v1 on v0

v1 whole, which is shorter than its diff:
```python
import functools

import jax
import jax.numpy as jnp
from jax import lax
from jax.experimental import pallas as pl
from jax.experimental.pallas import tpu as pltpu
from jax.sharding import PartitionSpec as P

DH = 128
CHIPS = 4
CORES = 2
LOG2E = 1.4426950408889634
NEG = -1e30
MESH = pl.DeviceIdType.MESH
BF = jnp.bfloat16
F32 = jnp.float32

DIRECT = (
    (0, 1, 0, 0),
    (0, 3, 0, 1),
    (0, 1, 0, 1),
    (0, 3, 0, 0),
    (1, 2, 1, 0),
    (1, 0, 1, 1),
    (1, 2, 1, 1),
    (2, 3, 2, 0),
    (2, 3, 2, 1),
)
RELAY = ((1, 2, 0, 0), (3, 2, 0, 1), (2, 3, 1, 0), (0, 3, 1, 1))
FIRST = (
    (3, 0, 1, 1, 0),
    (3, 2, 1, 0, 0),
    (3, 0, 0, 0, 2),
    (3, 2, 2, 0, 1),
    (3, 2, 2, 1, 2),
    (2, 1, 0, 0, 0),
    (2, 3, 0, 1, 0),
    (2, 1, 1, 1, 2),
    (1, 0, 0, 1, 3),
)
SECOND = ((3, 0, 0, 1, 4), (2, 1, 1, 0, 1), (1, 0, 0, 0, 1), (0, 1, 1, 1, 3))
FINAL = {
    0: ((0, (1, 2)), (1, (3, 4))),
    1: ((0, (1,)), (1, (2, 3))),
    2: ((0, (1,)), (1, (2,))),
    3: (),
}


def contract(a, b, dims):
    return lax.dot_general(a, b, ((dims[:1], dims[1:]), ((), ())), preferred_element_type=F32)


def kernel(
    tensor_count,
    dp_count,
    q_hbm,
    k_hbm,
    v_hbm,
    g_hbm,
    pos_ref,
    sink_ref,
    att_out,
    dq_out,
    dk_out,
    dv_out,
    sink_out,
    q_s,
    g_s,
    k_s,
    v_s,
    scores,
    probs,
    sgrad,
    pos_src,
    pos_all,
    pos_col,
    att_t,
    dq_t,
    att_s,
    dq_s,
    dk_f,
    dv_f,
    dk_b,
    dv_b,
    dk_r,
    dv_r,
    sink_src,
    sink_seq,
    sink_mid,
    sink_dp,
    in_send,
    in_recv,
    pos_send,
    pos_recv,
    gx_send,
    gx_recv,
    rx_send,
    rx_recv,
    out_send,
    out_recv,
    sink_send,
    sink_recv,
):
    seq = lax.axis_index("seq")
    dp = lax.axis_index("dp")
    t = lax.axis_index("tensor")
    x = lax.div(seq, CORES)
    c = lax.rem(seq, CORES)
    rows = q_hbm.shape[1]
    cap = rows * tensor_count
    slab = CORES * cap
    seq_count = CHIPS * CORES
    part = slab // 3

    peers = [(dc, dt) for dt in range(tensor_count) for dc in range(CORES)][1:]
    order = []
    for step in range(1, tensor_count // 2 + 1):
        for dt in (step, tensor_count - step):
            for dc in range(CORES):
                if (dc, dt) in peers and (dc, dt) not in order:
                    order.append((dc, dt))
    order = order + [p for p in peers if p not in order]

    def peer(dc, dt):
        return lax.rem(c + dc, CORES), lax.rem(t + dt, tensor_count)

    def seq_peer(d):
        return lax.rem(seq + d, seq_count)

    barrier = pltpu.get_barrier_semaphore()
    greeted = 0
    for dc, dt in order:
        if dt == 0:
            continue
        pc, pt = peer(dc, dt)
        pl.semaphore_signal(
            barrier, inc=1, device_id={"seq": x * CORES + pc, "tensor": pt}, device_id_type=MESH
        )
        greeted += 1
    for d in range(1, seq_count):
        pl.semaphore_signal(barrier, inc=1, device_id={"seq": seq_peer(d)}, device_id_type=MESH)
        greeted += 1
    for d in range(1, dp_count):
        pl.semaphore_signal(
            barrier, inc=1, device_id={"dp": lax.rem(dp + d, dp_count)}, device_id_type=MESH
        )
        greeted += 1

    pos_row = pos_ref[...]
    pos_src[...] = jnp.broadcast_to(pos_row, (8, cap))
    pos_all[seq] = jnp.broadcast_to(pos_row, (8, cap))
    pl.semaphore_wait(barrier, greeted)

    def remote(src, dst, send, recv, **where):
        return pltpu.make_async_remote_copy(
            src_ref=src, dst_ref=dst, send_sem=send, recv_sem=recv, device_id=where, device_id_type=MESH
        )

    def head_cols(pc, pt):
        return pl.ds(pl.multiple_of((pt * CORES + pc) * DH, DH), DH)

    def row_block(pc, pt):
        return pl.ds(pl.multiple_of(pc * cap + pt * rows, rows), rows)

    mine = row_block(c, t)

    def send_rows(n, src, dst):
        for dc, dt in order:
            pc, pt = peer(dc, dt)
            remote(
                src.at[0, :, head_cols(pc, pt)],
                dst.at[mine, :],
                in_send.at[n],
                in_recv.at[n],
                seq=x * CORES + pc,
                tensor=pt,
            ).start()
        pltpu.make_async_copy(
            src.at[0, :, head_cols(c, t)], dst.at[mine, :], in_recv.at[n]
        ).start()

    def pos_copy(d):
        return remote(
            pos_src, pos_all.at[seq], pos_send.at[d], pos_recv.at[d], seq=seq_peer(d)
        )

    send_rows(0, k_hbm, k_s.at[x])
    for d in range(1, seq_count):
        pos_copy(d).start()
    send_rows(1, v_hbm, v_s.at[x])
    send_rows(2, q_hbm, q_s)
    send_rows(3, g_hbm, g_s)

    def got_rows(n):
        pltpu.make_async_copy(q_s, q_s, in_recv.at[n]).wait()

    def half_rows(h):
        return pl.ds(h * cap, cap)

    def gather_copy(a, buf, n, move):
        _, to, j, h = move
        return remote(
            buf.at[j, half_rows(h), :],
            buf.at[j, half_rows(h), :],
            gx_send.at[a, n],
            gx_recv.at[a, j, h],
            seq=to * CORES + c,
        )

    def gather_wait(a, buf, j, h):
        ref = buf.at[j, half_rows(h), :]
        pltpu.make_async_copy(ref, ref, gx_recv.at[a, j, h]).wait()

    def gather_direct(a, buf):
        for i in range(CHIPS):

            @pl.when(x == i)
            def _():
                for n, move in enumerate(DIRECT):
                    if move[0] == i:
                        gather_copy(a, buf, n, move).start()

    def gather_relay(a, buf):
        for n, move in enumerate(RELAY):

            @pl.when(x == move[0])
            def _():
                gather_wait(a, buf, move[2], move[3])
                gather_copy(a, buf, len(DIRECT) + n, move).start()

    def gather_rest(a, buf):
        for i in range(CHIPS):
            relayed = [m[2:] for m in RELAY if m[0] == i]
            rest = [m[2:] for m in DIRECT + RELAY if m[1] == i and m[2:] not in relayed]
            if rest:

                @pl.when(x == i)
                def _():
                    for j, h in rest:
                        gather_wait(a, buf, j, h)

    got_rows(0)
    gather_direct(0, k_s)

    for d in range(1, seq_count):
        pltpu.make_async_copy(pos_src, pos_all.at[seq], pos_recv.at[d]).wait()

    def column(s, _):
        held = pos_all[s][:1, :]
        held = jnp.where(held < 0, jnp.int32(1 << 30), held)
        wide = jnp.broadcast_to(held, (DH, cap)).astype(F32)
        pos_col[pl.ds(pl.multiple_of(s * cap, cap), cap), :] = wide.T
        return 0

    lax.fori_loop(0, seq_count, column, 0)
    pos_q = jnp.concatenate(
        [pos_all[x * CORES][:1, :], pos_all[x * CORES + 1][:1, :]], axis=1
    ).astype(F32)

    got_rows(1)
    gather_direct(1, v_s)
    gather_relay(0, k_s)
    got_rows(2)

    sink2 = sink_ref[c] * LOG2E
    to_log2 = DH**-0.5 * LOG2E

    def score_block(b, carry):
        row_max, total = carry
        at = pl.ds(pl.multiple_of(b * part, part), part)
        j = lax.div(b, 3)
        inner = pl.ds(pl.multiple_of(lax.rem(b, 3) * part, part), part)
        s = contract(k_s[j, inner, :], q_s[...], (1, 1)) * to_log2
        pos_k = jnp.concatenate([pos_col[at, :]] * (slab // DH), axis=1)
        s = jnp.where(pos_k <= pos_q, s, NEG)
        scores[at, :] = s
        new_max = jnp.maximum(row_max, jnp.max(s, axis=0, keepdims=True))
        total = total * jnp.exp2(row_max - new_max) + jnp.sum(
            jnp.exp2(s - new_max), axis=0, keepdims=True
        )
        return new_max, total

    start = (jnp.full((1, slab), sink2, F32), jnp.ones((1, slab), F32))
    carry = lax.fori_loop(x * 3, x * 3 + 3, score_block, start)
    gather_relay(1, v_s)
    gather_rest(0, k_s)
    row_max, total = lax.fori_loop(0, x * 3, score_block, carry)
    lse = row_max + jnp.log2(total)

    gather_rest(1, v_s)
    att_t[...] = jnp.zeros_like(att_t)

    def attend_slab(j, _):
        def prob_block(i, _):
            at = pl.ds(pl.multiple_of(j * slab + i * part, part), part)
            probs[at, :] = jnp.exp2(scores[at, :] - lse).astype(BF)
            return 0

        lax.fori_loop(0, 3, prob_block, 0)
        whole = pl.ds(pl.multiple_of(j * slab, slab), slab)
        att_t[...] += contract(v_s[j], probs[whole, :], (0, 0))
        return 0

    lax.fori_loop(0, x + 1, attend_slab, 0)
    att_s[...] = att_t[...].T.astype(BF)

    def send_heads(n, src, dst):
        for dc, dt in order:
            pc, pt = peer(dc, dt)
            remote(
                src.at[row_block(pc, pt), :],
                dst.at[0, :, head_cols(c, t)],
                out_send.at[n],
                out_recv.at[n],
                seq=x * CORES + pc,
                tensor=pt,
            ).start()
        pltpu.make_async_copy(
            src.at[mine, :], dst.at[0, :, head_cols(c, t)], out_recv.at[n]
        ).start()

    send_heads(0, att_s, att_out)
    got_rows(3)

    delta = jnp.sum(
        att_s[...].astype(F32).T * g_s[...].astype(F32).T, axis=0, keepdims=True
    )

    own_sink = -jnp.sum(jnp.exp2(sink2 - lse) * delta)
    lane = lax.broadcasted_iota(jnp.int32, (8, DH), 1)
    own_tile = jnp.where(lane == c, own_sink, 0.0)
    sink_src[...] = own_tile
    sink_seq[seq] = own_tile

    def sink_seq_copy(d):
        return remote(
            sink_src, sink_seq.at[seq], sink_send.at[0, d], sink_recv.at[0, d], seq=seq_peer(d)
        )

    def sink_dp_copy(d):
        return remote(
            sink_mid,
            sink_dp.at[dp],
            sink_send.at[1, d],
            sink_recv.at[1, d],
            dp=lax.rem(dp + d, dp_count),
        )

    for d in range(1, seq_count):
        sink_seq_copy(d).start()

    def value_slab(j, _):
        whole = pl.ds(pl.multiple_of(j * slab, slab), slab)
        out = contract(probs[whole, :], g_s[...], (1, 0))
        dv_f[j] = out
        dv_b[j] = out.astype(BF)
        return 0

    lax.fori_loop(0, x + 1, value_slab, 0)

    def reduce_copy(a, buf, got, n, move):
        _, to, j, h, slot = move
        return remote(
            buf.at[j, half_rows(h), :],
            got.at[slot],
            rx_send.at[a, n],
            rx_recv.at[a, slot],
            seq=to * CORES + c,
        )

    def reduce_wait(a, got, slot):
        pltpu.make_async_copy(got.at[slot], got.at[slot], rx_recv.at[a, slot]).wait()

    def reduce_first(a, buf, got):
        for i in range(CHIPS):

            @pl.when(x == i)
            def _():
                for n, move in enumerate(FIRST):
                    if move[0] == i:
                        reduce_copy(a, buf, got, n, move).start()

    def reduce_second(a, own, buf, got):
        for n, move in enumerate(SECOND):
            i, to, j, h, slot = move

            @pl.when(x == i)
            def _():
                reduce_wait(a, got, 0)
                if i == 0:
                    buf[j, half_rows(h), :] = got[0]
                else:
                    buf[j, half_rows(h), :] = (
                        own[j, half_rows(h), :] + got[0].astype(F32)
                    ).astype(BF)
                reduce_copy(a, buf, got, len(FIRST) + n, move).start()

    def reduce_last(a, own, buf, got):
        for i in range(CHIPS):
            for h, slots in FINAL[i]:

                @pl.when(x == i)
                def _():
                    total = own[i, half_rows(h), :]
                    for slot in slots:
                        reduce_wait(a, got, slot)
                        total = total + got[slot].astype(F32)
                    buf[i, half_rows(h), :] = total.astype(BF)

    reduce_first(0, dv_b, dv_r)
    dq_t[...] = jnp.zeros_like(dq_t)

    def grad_slab(j, _):
        def grad_block(i, _):
            at = pl.ds(pl.multiple_of(j * slab + i * part, part), part)
            inner = pl.ds(pl.multiple_of(i * part, part), part)
            dots = contract(v_s[j, inner, :], g_s[...], (1, 1))
            sgrad[inner, :] = (jnp.exp2(scores[at, :] - lse) * (dots - delta)).astype(BF)
            return 0

        lax.fori_loop(0, 3, grad_block, 0)
        out = contract(sgrad[...], q_s[...], (1, 0)) * DH**-0.5
        dk_f[j] = out
        dk_b[j] = out.astype(BF)
        dq_t[...] += contract(k_s[j], sgrad[...], (0, 0))
        return 0

    lax.fori_loop(0, x + 1, grad_slab, 0)
    reduce_first(1, dk_b, dk_r)
    dq_s[...] = (dq_t[...] * DH**-0.5).T.astype(BF)
    send_heads(1, dq_s, dq_out)

    for d in range(1, seq_count):
        pltpu.make_async_copy(sink_src, sink_src, sink_recv.at[0, d]).wait()
    seq_sum = jnp.sum(sink_seq[...], axis=0)
    sink_mid[...] = seq_sum
    sink_dp[dp] = seq_sum
    for d in range(1, dp_count):
        sink_dp_copy(d).start()

    reduce_second(0, dv_f, dv_b, dv_r)
    reduce_last(0, dv_f, dv_b, dv_r)
    send_heads(3, dv_b.at[x], dv_out)
    reduce_second(1, dk_f, dk_b, dk_r)
    reduce_last(1, dk_f, dk_b, dk_r)
    send_heads(2, dk_b.at[x], dk_out)

    for d in range(1, dp_count):
        pltpu.make_async_copy(sink_mid, sink_mid, sink_recv.at[1, d]).wait()
    sink_out[...] = jnp.sum(sink_dp[...], axis=0)

    sent = q_s.at[pl.ds(0, slab - rows), :]
    for n in range(4):
        pltpu.make_async_copy(sent, sent, in_send.at[n]).wait()
        pltpu.make_async_copy(sent, sent, out_send.at[n]).wait()
        pltpu.make_async_copy(q_s, q_s, out_recv.at[n]).wait()
    for d in range(1, seq_count):
        pltpu.make_async_copy(pos_src, pos_src, pos_send.at[d]).wait()
        pltpu.make_async_copy(sink_src, sink_src, sink_send.at[0, d]).wait()
    for d in range(1, dp_count):
        pltpu.make_async_copy(sink_mid, sink_mid, sink_send.at[1, d]).wait()
    for i in range(CHIPS):

        @pl.when(x == i)
        def _():
            for a in range(2):
                half = k_s.at[0, half_rows(0), :]
                for n, move in enumerate(DIRECT + RELAY):
                    if move[0] == i:
                        pltpu.make_async_copy(half, half, gx_send.at[a, n]).wait()
                for n, move in enumerate(FIRST + SECOND):
                    if move[0] == i:
                        pltpu.make_async_copy(half, half, rx_send.at[a, n]).wait()


def on_device(queries, key_vectors, values, out_grad, positions, sink_logits):
    tensor_count = lax.axis_size("tensor")
    dp_count = lax.axis_size("dp")
    _, rows, features = queries.shape
    cap = rows * tensor_count
    slab = CORES * cap
    seq_count = CHIPS * CORES
    hbm = pl.BlockSpec(memory_space=pl.ANY)
    vmem = pl.BlockSpec(memory_space=pltpu.VMEM)
    smem = pl.BlockSpec(memory_space=pltpu.SMEM)
    row_type = jax.ShapeDtypeStruct((1, rows, features), BF)
    dma = pltpu.SemaphoreType.DMA
    moves = len(DIRECT) + len(RELAY)
    hops = len(FIRST) + len(SECOND)
    outs = pl.pallas_call(
        functools.partial(kernel, tensor_count, dp_count),
        out_shape=(row_type,) * 4 + (jax.ShapeDtypeStruct((8, DH), F32),),
        in_specs=[hbm] * 4 + [vmem, smem],
        out_specs=(hbm,) * 4 + (vmem,),
        scratch_shapes=[
            pltpu.VMEM((slab, DH), BF),
            pltpu.VMEM((slab, DH), BF),
            pltpu.VMEM((CHIPS, slab, DH), BF),
            pltpu.VMEM((CHIPS, slab, DH), BF),
            pltpu.VMEM((CHIPS * slab, slab), F32),
            pltpu.VMEM((CHIPS * slab, slab), BF),
            pltpu.VMEM((slab, slab), BF),
            pltpu.VMEM((8, cap), jnp.int32),
            pltpu.VMEM((seq_count, 8, cap), jnp.int32),
            pltpu.VMEM((seq_count * cap, DH), F32),
            pltpu.VMEM((DH, slab), F32),
            pltpu.VMEM((DH, slab), F32),
            pltpu.VMEM((slab, DH), BF),
            pltpu.VMEM((slab, DH), BF),
            pltpu.VMEM((CHIPS, slab, DH), F32),
            pltpu.VMEM((CHIPS, slab, DH), F32),
            pltpu.VMEM((CHIPS, slab, DH), BF),
            pltpu.VMEM((CHIPS, slab, DH), BF),
            pltpu.VMEM((5, cap, DH), BF),
            pltpu.VMEM((5, cap, DH), BF),
            pltpu.VMEM((8, DH), F32),
            pltpu.VMEM((seq_count, 8, DH), F32),
            pltpu.VMEM((8, DH), F32),
            pltpu.VMEM((dp_count, 8, DH), F32),
            dma((4,)),
            dma((4,)),
            dma((seq_count,)),
            dma((seq_count,)),
            dma((2, moves)),
            dma((2, CHIPS, 2)),
            dma((2, hops)),
            dma((2, 5)),
            dma((4,)),
            dma((4,)),
            dma((2, max(seq_count, dp_count))),
            dma((2, max(seq_count, dp_count))),
        ],
        compiler_params=pltpu.CompilerParams(
            collective_id=0, has_side_effects=True, vmem_limit_bytes=48 * 1024 * 1024
        ),
        name="routed_attention",
    )(queries, key_vectors, values, out_grad, positions, sink_logits)
    return (*outs[:4], outs[4][0, :CORES])


def solution(mesh):
    rows = P("dp", ("seq", "tensor"), None)
    return jax.shard_map(
        on_device,
        mesh=mesh,
        in_specs=(rows, rows, rows, rows, P("dp", "seq"), P("tensor")),
        out_specs=(rows, rows, rows, rows, P("tensor")),
        check_vma=False,
    )
```

time: 255 us -> 79.4 us (0.31)
  Pallas kernels: 0 us -> 70.2 us
  starting transfers between devices: 61 us -> 0 us
  blocking collectives: 56.9 us -> 0 us
  local copies, waits for them, and re-layouts: 52.1 us -> 8.25 us
  matrix products: 31.5 us -> 0 us
  waiting for transfers between devices: 27.6 us -> 0 us
  between operations: 14.1 us -> 0.66 us
  other arithmetic: 9.84 us -> 0 us
    pallas_call x0 -> x1, Pallas kernels: none -> 70.2 us  [on_device(): pl.pallas_call(functools.partial(kernel, tensor_count, dp_count), out_sha...]
    all_to_all x3 -> x0, starting transfers between devices: 60.8 us -> none  [the longest x1 47.8 us: sent_to_all(): return lax.all_to_all(copies, axis, split_axis=0, concat_axis=0, tiled=True)]
    dot_general x16 -> x0, matrix products: 31.5 us -> none  [the longest x6 10.5 us: block_scores(): jnp.einsum('ghd,khd->hgk', query_block, key_block, preferred_element_type...]
    all_gather x2 -> x0, blocking collectives: 29.2 us -> none  [the longest x1 15.7 us: on_device(): lax.all_gather(pos_rows, 'seq', axis=0, tiled=True)]
    all_to_all x1 -> x0, blocking collectives: 27.7 us -> none  [sent_together(): lax.all_to_all(both, axis, split_axis=split_dim, concat_axis=concat_dim,...]
    dynamic_slice x18 -> x0, local copies, waits for them, and re-layouts: 17 us -> none  [the longest x4 6.65 us: key_one_block(): lax.dynamic_slice_in_dim(grad_all, block * query_span, query_span, 0)]
    all_gather x3 -> x0, waiting for transfers between devices: 16.5 us -> none  [the longest x1 16.4 us: in_one_piece(): lax.all_gather(both, axis, axis=dim, tiled=True)]
    all_to_all x3 -> x0, waiting for transfers between devices: 11.1 us -> none  [the longest x2 11.1 us: sent_together(): lax.all_to_all(both, axis, split_axis=split_dim, concat_axis=concat_dim,...]
  transfers between devices with their start and end apart: 6 -> 0, of which waited for: 2 -> 0; matrix products, arithmetic and copies ran while one was open for 30% -> 0% of each run, Pallas kernels for 0% -> 0%
where the time goes in v1:
time: 79.4 us; the launch traced here: 79.1 us
  Pallas kernels  70.2 us (88%)
  local copies, waits for them, and re-layouts  8.25 us (10%)
    pallas_call x1, Pallas kernels, on_device(): pl.pallas_call(functools.partial(kernel, tensor_count, dp_count), out_sha...  70.2 us
    unnamed x16, local copies, waits for them, and re-layouts  7.74 us

profile of v1, /device:TPU:1, one launch (start us, length us, event | category | flops | bytes accessed | tf_op | source)
XLA Modules:
  0.0 79.1 jit_solution(16352030373496373013)
XLA Ops:
  0.6 0.0 copy-start
  0.6 0.9 %copy-done = bf16[1,48,2048]{2,1,0:T(8,128)(2,1)S(1)} copy-done((bf16[1,48,2048]{2,1,0:T(8,128)(2,1)S(1)}, bf16[1,48,2048]{2,1,0:T(8,128)(2,1)}, u32[]{:S(2)}) %copy-start) | copy-done | bytes 196632
  1.6 0.0 copy-start.1
  1.6 0.9 %copy-done.1 = bf16[1,48,2048]{2,1,0:T(8,128)(2,1)S(1)} copy-done((bf16[1,48,2048]{2,1,0:T(8,128)(2,1)S(1)}, bf16[1,48,2048]{2,1,0:T(8,128)(2,1)}, u32[]{:S(2)}) %copy-start.1) | copy-done | bytes 196632
  2.5 0.0 copy-start.2
  2.5 0.9 %copy-done.2 = bf16[1,48,2048]{2,1,0:T(8,128)(2,1)S(1)} copy-done((bf16[1,48,2048]{2,1,0:T(8,128)(2,1)S(1)}, bf16[1,48,2048]{2,1,0:T(8,128)(2,1)}, u32[]{:S(2)}) %copy-start.2) | copy-done | bytes 196632
  3.4 0.0 copy-start.3
  3.4 0.9 %copy-done.3 = bf16[1,48,2048]{2,1,0:T(8,128)(2,1)S(1)} copy-done((bf16[1,48,2048]{2,1,0:T(8,128)(2,1)S(1)}, bf16[1,48,2048]{2,1,0:T(8,128)(2,1)}, u32[]{:S(2)}) %copy-start.3) | copy-done | bytes 196632
  4.3 0.0 copy-start.4
  4.3 0.7 copy-done.4
  5.0 0.0 copy-start.5
  5.0 0.7 copy-done.5
  5.7 70.2 %routed_attention.1 = (bf16[1,48,2048]{2,1,0:T(8,128)(2,1)S(1)}, bf16[1,48,2048]{2,1,0:T(8,128)(2,1)S(1)}, bf16[1,48,2048]{2,1,0:T(8,128)(2,1)S(1)}, bf16[1,48,2048]{2,1,0:T(8,128)(2,1)S(1)}, f32[8,128]{1,0:T(8,128)S(1)}) custom-call(bf16[1,48,2048]{2,1,0:T(8,128)(2,1)S(1)} %copy-done, bf16[1,48,2048]{2,1,0:T(8,128)(2,1)S(1)} %copy-done.1, ...), custom_call_target="tpu_custom_call" | custom-call | tf_op jit(solution)/shard_map/routed_attention/pallas_call | solution.py:492
  75.9 0.5 slice_bitcast_fusion
  76.4 0.7 copy.15
  77.1 0.7 copy.16
  77.8 0.7 copy.17
  78.4 0.7 copy.18
Async XLA Ops:
  0.6 0.9 %copy-start = (bf16[1,48,2048]{2,1,0:T(8,128)(2,1)S(1)}, bf16[1,48,2048]{2,1,0:T(8,128)(2,1)}, u32[]{:S(2)}) copy-start(bf16[1,48,2048]{2,1,0:T(8,128)(2,1)} %q_hbm.1) | copy-start | bytes 589828
  1.6 0.9 %copy-start.1 = (bf16[1,48,2048]{2,1,0:T(8,128)(2,1)S(1)}, bf16[1,48,2048]{2,1,0:T(8,128)(2,1)}, u32[]{:S(2)}) copy-start(bf16[1,48,2048]{2,1,0:T(8,128)(2,1)} %k_hbm.1) | copy-start | bytes 589828
  2.5 0.9 %copy-start.2 = (bf16[1,48,2048]{2,1,0:T(8,128)(2,1)S(1)}, bf16[1,48,2048]{2,1,0:T(8,128)(2,1)}, u32[]{:S(2)}) copy-start(bf16[1,48,2048]{2,1,0:T(8,128)(2,1)} %v_hbm.1) | copy-start | bytes 589828
  3.4 0.9 %copy-start.3 = (bf16[1,48,2048]{2,1,0:T(8,128)(2,1)S(1)}, bf16[1,48,2048]{2,1,0:T(8,128)(2,1)}, u32[]{:S(2)}) copy-start(bf16[1,48,2048]{2,1,0:T(8,128)(2,1)} %g_hbm.1) | copy-start | bytes 589828
  4.3 0.7 copy-start.4
  5.0 0.7 copy-start.5
